TPU v7x, 16 devices: a whole 2x2x2 slice. The times are simulated.
16 devices in a mesh: frag: 2 (over z), dev: 8 (over y, x, core).
Axes of the slice: x: 2, y: 2, z: 2, core: 2. Of those that a mesh axis runs over, the one named last changes fastest.
Arguments:
- ao_ints: bfloat16 [192, 96, 96, 96], P(('frag', 'dev')), parts along dimension 0
- coeffs: bfloat16 [192, 96], P('frag'), parts along dimension 0
Outputs:
- output: float32 [192, 96, 9216], P('frag', None, 'dev'), parts along dimension 0
There are 2 independent parts. A program takes and returns all parts, laid end to end along the dimension named above; each array names one.
All inputs are finite; a program needn't handle non-finite values.
Results may differ from a plain program's by a relative error of at most 0.001.
Values are sent between devices in bfloat16 or wider.
A program may use at most 1 GiB of HBM per device.

v0:
```python
import functools

import jax
import jax.numpy as jnp
from jax import lax
from jax.experimental import pallas as pl
from jax.experimental.pallas import tpu as pltpu
from jax.sharding import PartitionSpec as P


PIECES = ((0, 1, (1152,)), (1, 1, (1152,)), (2, 2, (1152,)), (4, 3, (1152,)), (7, 5, (512, 512, 128)))
TILES = ((0, 512, 32, 1), (512, 512, 32, 1), (1024, 128, 32, 2))
F32, BF16 = jnp.float32, jnp.bfloat16


def one_hot(shape, fn):
    rows = lax.broadcasted_iota(jnp.int32, shape, 0)
    cols = lax.broadcasted_iota(jnp.int32, shape, 1)
    return fn(rows, cols)


def dot(a, b):
    return jnp.dot(a, b, preferred_element_type=F32)


def pick(shape, fn):
    return one_hot(shape, fn).astype(BF16)


def transposed(c, n):
    eye = pick((n, n), lambda i, j: i == j)
    return lax.dot_general(c, eye, (((0,), (0,)), ((), ())), preferred_element_type=F32).astype(BF16)


def build_first(n, c_ref, l1_ref, r2_ref, ct_ref):
    c = c_ref[...]
    ct = transposed(c, n)
    ct_ref[...] = ct
    tall = dot(pick((8 * n, n), lambda i, j: i // 8 == j), ct).astype(BF16)
    wide = dot(tall, pick((n, 8 * n), lambda i, j: j % n == i))
    keep = one_hot((8 * n, 8 * n), lambda i, j: i % 8 == j // n)
    l1_ref[...] = jnp.where(keep, wide, 0.0).astype(BF16)
    tall = dot(pick((512, n), lambda i, j: i % 128 == j), c).astype(BF16)
    wide = dot(tall, pick((n, 4 * n), lambda i, j: j % n == i))
    keep = one_hot((512, 4 * n), lambda i, j: i // 128 == j // n)
    r2_ref[...] = jnp.where(keep, wide, 0.0).astype(BF16)


def build_last(n, rows, me, ct_ref, l4_ref):
    def source(r, col):
        m = col // 8
        return r == (me ^ (m // rows)) * rows + m % rows

    tall = dot(pick((8 * n, n), lambda i, j: i // 8 == j), ct_ref[...]).astype(BF16)
    wide = dot(tall, pick((n, 8 * n), source))
    keep = one_hot((8 * n, 8 * n), lambda i, j: i % 8 == j % 8)
    l4_ref[...] = jnp.where(keep, wide, 0.0).astype(BF16)


def one_row(n, n_dev, tiles, me, a_ref, l1_ref, r2_ref, ct_ref, outs, t1_ref):
    nj = n // n_dev
    zero = jnp.zeros((8 * n, 128 - n), BF16)

    def first(g, carry):
        q0 = pl.multiple_of(g * 16, 16)
        lo = a_ref[pl.ds(q0, 8)].reshape(8 * n, n)
        hi = a_ref[pl.ds(q0 + 8, 8)].reshape(8 * n, n)
        t = dot(l1_ref[...], jnp.concatenate([lo, zero, hi, zero], axis=1))
        both = jnp.concatenate([t[:, :128].reshape(n, 8, 128), t[:, 128:].reshape(n, 8, 128)], axis=1)
        t1_ref[:, pl.ds(q0, 16), :] = both.astype(BF16)
        return carry

    lax.fori_loop(0, n // 16, first, 0)
    for k in range(n_dev):
        d = me ^ k
        t = t1_ref[pl.ds(d * nj, nj)].reshape(nj // 4, 4, n, 128)
        lhs = jnp.concatenate([t[:, jj].reshape(nj // 4 * n, 128) for jj in range(4)], axis=1)
        h = dot(lhs, r2_ref[...]).astype(BF16)
        h = jnp.concatenate([h[g * n:(g + 1) * n] for g in range(nj // 4)], axis=1)
        g = dot(ct_ref[...], h).astype(BF16)
        off = 0
        for t_i, w in enumerate(tiles):
            outs[k * len(tiles) + t_i][0] = g[:, off:off + w]
            off += w


def first_kernel(n, n_dev, tiles, me_ref, a_hbm, c_ref, l1_ref, r2_ref, ct_ref, *rest):
    outs, (a_buf, t1_ref, sem) = rest[:-3], rest[-3:]
    copy = pltpu.make_async_copy(a_hbm.at[0], a_buf, sem)
    copy.start()
    build_first(n, c_ref, l1_ref, r2_ref, ct_ref)
    copy.wait()
    one_row(n, n_dev, tiles, me_ref[0], a_buf, l1_ref, r2_ref, ct_ref, outs, t1_ref)


def send_kernel(n, n_dev, rows, tiles, last, me_ref, a_ref, l1_ref, r2_ref, ct_ref, before, *rest):
    outs, t1_ref = rest[:n_dev * len(tiles)], rest[-1]
    one_row(n, n_dev, tiles, me_ref[0], a_ref.at[0], l1_ref, r2_ref, ct_ref, outs, t1_ref)
    if last:
        @pl.when(pl.program_id(0) == 0)
        def _():
            build_last(n, rows, me_ref[0], ct_ref, rest[-2])


def out_kernel(n, n_in, width, depth, pack, *refs):
    l4_ref, out_ref = refs[n_in], refs[-1]
    ins = refs[:n_in]

    def step(s, carry):
        a0 = pl.multiple_of(s * 8 * pack, 8 * pack)
        cols = []
        for x in range(pack):
            cols.append(jnp.concatenate(
                [r[:, pl.ds(a0 + 8 * x, 8), :].reshape(-1, width) for r in ins], axis=0))
        rhs = cols[0] if pack == 1 else jnp.concatenate(cols, axis=1)
        v = dot(l4_ref[...], rhs)
        for x in range(pack):
            out_ref[:, pl.ds(a0 + 8 * x, 8), :] = v[:, x * width:(x + 1) * width].reshape(n, 8, width)
        return carry

    lax.fori_loop(0, depth // (8 * pack), step, 0)


def solution(mesh):
    n_dev = mesh.shape['dev']

    def transform(ao_rows, coeffs):
        rows = ao_rows.shape[0]
        n = coeffs.shape[0]
        wide = n * n // n_dev
        me_arr = jnp.full((1,), lax.axis_index('dev'), jnp.int32)
        smem = pl.BlockSpec(memory_space=pltpu.SMEM)
        vmem = pl.BlockSpec(memory_space=pltpu.VMEM)
        hbm = pl.BlockSpec(memory_space=pl.ANY)

        def const(shape):
            return pl.BlockSpec(shape, lambda *_: (0,) * len(shape))

        square, second = (8 * n, 8 * n), (512, 4 * n)
        got = [[] for _ in range(n_dev)]
        for i, (p0, count, tiles) in enumerate(PIECES):
            block_specs = [pl.BlockSpec((1, n, w), lambda i: (i, 0, 0)) for _ in range(n_dev) for w in tiles]
            block_shapes = [jax.ShapeDtypeStruct((count, n, w), BF16) for _ in range(n_dev) for w in tiles]
            t1 = pltpu.VMEM((n, n, 128), BF16)
            if i == 0:
                l1, r2, ct, *sent = pl.pallas_call(
                    functools.partial(first_kernel, n, n_dev, tiles),
                    grid=(1,),
                    in_specs=[smem, hbm, vmem],
                    out_specs=[const(square), const(second), const((n, n))] + block_specs,
                    out_shape=[jax.ShapeDtypeStruct(s, BF16) for s in (square, second, (n, n))] + block_shapes,
                    scratch_shapes=[pltpu.VMEM((n, n, n), BF16), t1, pltpu.SemaphoreType.DMA],
                    name='first',
                )(me_arr, ao_rows, coeffs)
            else:
                last = i == 1
                sent = pl.pallas_call(
                    functools.partial(send_kernel, n, n_dev, rows, tiles, last),
                    grid=(count,),
                    in_specs=[smem, pl.BlockSpec((1, n, n, n), lambda i, p0=p0: (p0 + i, 0, 0, 0)),
                              const(square), const(second), const((n, n)), hbm],
                    out_specs=block_specs + [const(square)] * last,
                    out_shape=block_shapes + [jax.ShapeDtypeStruct(square, BF16)] * last,
                    scratch_shapes=[t1],
                    name='send',
                )(me_arr, ao_rows, l1, r2, ct, before)
                if last:
                    l4 = sent[-1]
            before = sent[0]
            for t_i in range(len(tiles)):
                for k in range(n_dev):
                    block = sent[k * len(tiles) + t_i]
                    if k:
                        block = lax.ppermute(block, 'dev', [(i, i ^ k) for i in range(n_dev)])
                    got[k].append((block, t_i if len(tiles) > 1 else None))

        out = None
        for t_i, (off, w, depth, pack) in enumerate(TILES):
            ins, specs = [], []
            for k in range(n_dev):
                for block, tile in got[k]:
                    if tile in (None, t_i):
                        lane = off // w if tile is None else 0
                        ins.append(block)
                        specs.append(pl.BlockSpec((block.shape[0], depth, w), lambda i, lane=lane: (0, i, lane)))
            n_in = len(ins)
            ins.append(l4)
            specs.append(const(square))
            if out is not None:
                ins.append(out)
                specs.append(hbm)
            out = pl.pallas_call(
                functools.partial(out_kernel, n, n_in, w, depth, pack),
                grid=(n // depth,),
                in_specs=specs,
                out_specs=pl.BlockSpec((n, depth, w), lambda i, off=off, w=w: (0, i, off // w)),
                out_shape=jax.ShapeDtypeStruct((n, n, wide), F32),
                input_output_aliases={} if t_i == 0 else {len(ins) - 1: 0},
                name='out',
            )(*ins)
        return out

    return jax.shard_map(transform, mesh=mesh, in_specs=(P(('frag', 'dev')), P('frag')), out_specs=P('frag', None, 'dev'), check_vma=False)
```

profile of v0, /device:TPU:0, one launch (start us, length us, event | category | flops | bytes accessed | tf_op | source)
XLA Modules:
  0.0 380.5 jit_solution(17559458492698243416)
XLA Ops:
  0.0 8.8 %first.1 = (bf16[768,768]{1,0:T(8,128)(2,1)}, bf16[512,384]{1,0:T(8,128)(2,1)}, bf16[96,96]{1,0:T(8,128)(2,1)}, bf16[1,96,1152]{2,1,0:T(8,128)(2,1)}, bf16[1,96,...) custom-call(s32[1]{0:T(128)} %bitcast.me_ref, ...), custom_call_target="tpu_custom_call" | custom-call | tf_op jit(solution)/shard_map/first/pallas_call | solution.py:146
  12.1 9.2 %send.4 = (bf16[1,96,1152]{2,1,0:T(8,128)(2,1)}, bf16[1,96,1152]{2,1,0:T(8,128)(2,1)}, bf16[1,96,1152]{2,1,0:T(8,128)(2,1)}, bf16[1,96,1152]{2,1,0:T(8,128)(2,1)...) custom-call(s32[1]{0:T(128)} %bitcast.me_ref, ...), custom_call_target="tpu_custom_call" | custom-call | tf_op jit(solution)/shard_map/send/pallas_call | solution.py:157
  21.3 14.4 %send.5 = (bf16[2,96,1152]{2,1,0:T(8,128)(2,1)}, bf16[2,96,1152]{2,1,0:T(8,128)(2,1)}, bf16[2,96,1152]{2,1,0:T(8,128)(2,1)}, bf16[2,96,1152]{2,1,0:T(8,128)(2,1)...) custom-call(s32[1]{0:T(128)} %bitcast.me_ref, ...), custom_call_target="tpu_custom_call" | custom-call | tf_op jit(solution)/shard_map/send/pallas_call | solution.py:157
  35.7 20.1 %send.6 = (bf16[3,96,1152]{2,1,0:T(8,128)(2,1)}, bf16[3,96,1152]{2,1,0:T(8,128)(2,1)}, bf16[3,96,1152]{2,1,0:T(8,128)(2,1)}, bf16[3,96,1152]{2,1,0:T(8,128)(2,1)...) custom-call(s32[1]{0:T(128)} %bitcast.me_ref, ...), custom_call_target="tpu_custom_call" | custom-call | tf_op jit(solution)/shard_map/send/pallas_call | solution.py:157
  55.8 31.9 %send.7 = (bf16[5,96,512]{2,1,0:T(8,128)(2,1)}, bf16[5,96,512]{2,1,0:T(8,128)(2,1)}, bf16[5,96,128]{2,1,0:T(8,128)(2,1)}, bf16[5,96,512]{2,1,0:T(8,128)(2,1)}, b...) custom-call(s32[1]{0:T(128)} %bitcast.me_ref, ...), custom_call_target="tpu_custom_call" | custom-call | tf_op jit(solution)/shard_map/send/pallas_call | solution.py:157
  99.5 12.6 %collective-permute-done.20.refs_25_ = bf16[1,96,1152]{2,1,0:T(8,128)(2,1)S(1)} collective-permute-done((bf16[1,96,1152]{2,1,0:T(8,128)(2,1)S(1)}, bf16[1,96,1152]{2,1,0:T(8,128)(2,1)S(1)}, u32[]{:S(2)}, u32[]{:S(2)}) %collective-permute-start.20) | collective-permute-done | bytes 221216 | tf_op jit(solution)/shard_map/ppermute | solution.py:174
  116.3 3.5 collective-permute-done.11.refs_16_
  124.1 3.1 collective-permute-start.31
  127.1 18.0 %collective-permute-done.26.refs_31_ = bf16[1,96,1152]{2,1,0:T(8,128)(2,1)S(1)} collective-permute-done((bf16[1,96,1152]{2,1,0:T(8,128)(2,1)}, bf16[1,96,1152]{2,1,0:T(8,128)(2,1)S(1)}, u32[]{:S(2)}, u32[]{:S(2)}) %collective-permute-start.26) | collective-permute-done | bytes 221216 | tf_op jit(solution)/shard_map/ppermute | solution.py:174
  145.7 3.7 collective-permute-done.31.refs_36_
  152.4 25.7 %collective-permute-done.17.refs_22_ = bf16[2,96,1152]{2,1,0:T(8,128)(2,1)S(1)} collective-permute-done((bf16[2,96,1152]{2,1,0:T(8,128)(2,1)}, bf16[2,96,1152]{2,1,0:T(8,128)(2,1)S(1)}, u32[]{:S(2)}, u32[]{:S(2)}) %collective-permute-start.17) | collective-permute-done | bytes 442400 | tf_op jit(solution)/shard_map/ppermute | solution.py:174
  178.6 8.8 %collective-permute-done.22.refs_27_ = bf16[2,96,1152]{2,1,0:T(8,128)(2,1)S(1)} collective-permute-done((bf16[2,96,1152]{2,1,0:T(8,128)(2,1)}, bf16[2,96,1152]{2,1,0:T(8,128)(2,1)S(1)}, u32[]{:S(2)}, u32[]{:S(2)}) %collective-permute-start.22) | collective-permute-done | bytes 442400 | tf_op jit(solution)/shard_map/ppermute | solution.py:174
  192.1 9.0 %collective-permute-done.37.refs_19_ = bf16[5,96,512]{2,1,0:T(8,128)(2,1)S(1)} collective-permute-done((bf16[5,96,512]{2,1,0:T(8,128)(2,1)}, bf16[5,96,512]{2,1,0:T(8,128)(2,1)S(1)}, u32[]{:S(2)}, u32[]{:S(2)}) %collective-permute-start.37) | collective-permute-done | bytes 491552 | tf_op jit(solution)/shard_map/ppermute | solution.py:174
  202.7 19.7 %collective-permute-done.38.refs_24_ = bf16[5,96,512]{2,1,0:T(8,128)(2,1)S(1)} collective-permute-done((bf16[5,96,512]{2,1,0:T(8,128)(2,1)}, bf16[5,96,512]{2,1,0:T(8,128)(2,1)S(1)}, u32[]{:S(2)}, u32[]{:S(2)}) %collective-permute-start.38) | collective-permute-done | bytes 491552 | tf_op jit(solution)/shard_map/ppermute | solution.py:174
  224.6 7.7 %collective-permute-done.39.refs_29_ = bf16[5,96,512]{2,1,0:T(8,128)(2,1)S(1)} collective-permute-done((bf16[5,96,512]{2,1,0:T(8,128)(2,1)}, bf16[5,96,512]{2,1,0:T(8,128)(2,1)S(1)}, u32[]{:S(2)}, u32[]{:S(2)}) %collective-permute-start.39) | collective-permute-done | bytes 491552 | tf_op jit(solution)/shard_map/ppermute | solution.py:174
  236.8 9.0 %collective-permute-done.44.refs_19_ = bf16[5,96,512]{2,1,0:T(8,128)(2,1)S(1)} collective-permute-done((bf16[5,96,512]{2,1,0:T(8,128)(2,1)}, bf16[5,96,512]{2,1,0:T(8,128)(2,1)S(1)}, u32[]{:S(2)}, u32[]{:S(2)}) %collective-permute-start.44) | collective-permute-done | bytes 491552 | tf_op jit(solution)/shard_map/ppermute | solution.py:174
  249.4 7.5 %collective-permute-done.46.refs_29_ = bf16[5,96,512]{2,1,0:T(8,128)(2,1)S(1)} collective-permute-done((bf16[5,96,512]{2,1,0:T(8,128)(2,1)}, bf16[5,96,512]{2,1,0:T(8,128)(2,1)S(1)}, u32[]{:S(2)}, u32[]{:S(2)}) %collective-permute-start.46) | collective-permute-done | bytes 491552 | tf_op jit(solution)/shard_map/ppermute | solution.py:174
  258.1 13.3 %collective-permute-done.47.refs_34_ = bf16[5,96,512]{2,1,0:T(8,128)(2,1)S(1)} collective-permute-done((bf16[5,96,512]{2,1,0:T(8,128)(2,1)}, bf16[5,96,512]{2,1,0:T(8,128)(2,1)S(1)}, u32[]{:S(2)}, u32[]{:S(2)}) %collective-permute-start.47) | collective-permute-done | bytes 491552 | tf_op jit(solution)/shard_map/ppermute | solution.py:174
  273.2 7.9 %collective-permute-done.48.refs_39_ = bf16[5,96,512]{2,1,0:T(8,128)(2,1)S(1)} collective-permute-done((bf16[5,96,512]{2,1,0:T(8,128)(2,1)}, bf16[5,96,512]{2,1,0:T(8,128)(2,1)S(1)}, u32[]{:S(2)}, u32[]{:S(2)}) %collective-permute-start.48) | collective-permute-done | bytes 491552 | tf_op jit(solution)/shard_map/ppermute | solution.py:174
  284.3 11.0 %collective-permute-done.13.refs_18_ = bf16[3,96,1152]{2,1,0:T(8,128)(2,1)S(1)} collective-permute-done((bf16[3,96,1152]{2,1,0:T(8,128)(2,1)}, bf16[3,96,1152]{2,1,0:T(8,128)(2,1)S(1)}, u32[]{:S(2)}, u32[]{:S(2)}) %collective-permute-start.13) | collective-permute-done | bytes 663584 | tf_op jit(solution)/shard_map/ppermute | solution.py:174
  298.0 39.8 %collective-permute-done.23.refs_28_ = bf16[3,96,1152]{2,1,0:T(8,128)(2,1)S(1)} collective-permute-done((bf16[3,96,1152]{2,1,0:T(8,128)(2,1)}, bf16[3,96,1152]{2,1,0:T(8,128)(2,1)S(1)}, u32[]{:S(2)}, u32[]{:S(2)}) %collective-permute-start.23) | collective-permute-done | bytes 663584 | tf_op jit(solution)/shard_map/ppermute | solution.py:174
  342.1 15.7 %out.3.refs_41_ = f32[96,96,1152]{2,1,0:T(8,128)} custom-call(bf16[1,96,1152]{2,1,0:T(8,128)(2,1)} %get-tuple-element.65.before.refs_0_, bf16[1,96,1152]{2,1,0:T(8,128)(2,1)} %get-tuple-element.69.before.refs_1_, bf16[2,96,1152]{2,1,0:T(8,128)(2,1)} %get-tuple-element.70.before.refs_2_, bf16[3,96,1152]{2,1,0:T(8,128)(2,1)} %get-tuple-element.71.before.refs_3_, ...), custom_call_target="tpu_custom_call" | custom-call | tf_op jit(solution)/shard_map/out/pallas_call | solution.py:192
  357.8 15.7 %out.4.refs_41_ = f32[96,96,1152]{2,1,0:T(8,128)} custom-call(bf16[1,96,1152]{2,1,0:T(8,128)(2,1)} %get-tuple-element.65.before.refs_0_, bf16[1,96,1152]{2,1,0:T(8,128)(2,1)} %get-tuple-element.69.before.refs_1_, bf16[2,96,1152]{2,1,0:T(8,128)(2,1)} %get-tuple-element.70.before.refs_2_, ...), custom_call_target="tpu_custom_call", output_to_operand_aliasing={{}: (41, {})} | custom-call | tf_op jit(solution)/shard_map/out/pallas_call | solution.py:192
  373.6 6.7 %out.5 = f32[96,96,1152]{2,1,0:T(8,128)} custom-call(bf16[1,96,1152]{2,1,0:T(8,128)(2,1)} %get-tuple-element.65.before.refs_0_, bf16[1,96,1152]{2,1,0:T(8,128)(2,1)} %get-tuple-element.69.before.refs_1_, bf16[2,96,1152]{2,1,0:T(8,128)(2,1)} %get-tuple-element.70.before.refs_2_, ...), custom_call_target="tpu_custom_call", output_to_operand_aliasing={{}: (41, {})} | custom-call | tf_op jit(solution)/shard_map/out/pallas_call | solution.py:192
  (182 shorter events, 57.3 us)
Async XLA Ops:
  8.8 86.2 %collective-permute-start = (bf16[1,96,1152]{2,1,0:T(8,128)(2,1)}, bf16[1,96,1152]{2,1,0:T(8,128)(2,1)S(1)}, u32[]{:S(2)}, u32[]{:S(2)}) collective-permute-start(bf16[1,96,1152]{2,1,0:T(8,128)(2,1)} %get-tuple-element.73), channel_id=1, source_target_pairs={{0,1},{1,0},{2,3},{3,2},{4,5},{5,4},{6,7},{7,6},{8,9},{9,8},{10,11... | collective-permute-start | bytes 663560 | tf_op jit(solution)/shard_map/ppermute | solution.py:174
  9.6 87.0 %collective-permute-start.5 = (bf16[1,96,1152]{2,1,0:T(8,128)(2,1)}, bf16[1,96,1152]{2,1,0:T(8,128)(2,1)S(1)}, u32[]{:S(2)}, u32[]{:S(2)}) collective-permute-start(bf16[1,96,1152]{2,1,0:T(8,128)(2,1)} %get-tuple-element.78), channel_id=1, source_target_pairs={{0,2},{1,3},{2,0},{3,1},{4,6},{5,7},{6,4},{7,5},{8,10},{9,11},{10,... | collective-permute-start | bytes 663560 | tf_op jit(solution)/shard_map/ppermute | solution.py:174
  114.1 35.5 %collective-permute-start.2 = (bf16[2,96,1152]{2,1,0:T(8,128)(2,1)}, bf16[2,96,1152]{2,1,0:T(8,128)(2,1)S(1)}, u32[]{:S(2)}, u32[]{:S(2)}) collective-permute-start(bf16[2,96,1152]{2,1,0:T(8,128)(2,1)} %get-tuple-element.75), channel_id=1, source_target_pairs={{0,1},{1,0},{2,3},{3,2},{4,5},{5,4},{6,7},{7,6},{8,9},{9,8},{10,11... | collective-permute-start | bytes 1327112 | tf_op jit(solution)/shard_map/ppermute | solution.py:174
  114.5 35.3 %collective-permute-start.7 = (bf16[2,96,1152]{2,1,0:T(8,128)(2,1)}, bf16[2,96,1152]{2,1,0:T(8,128)(2,1)S(1)}, u32[]{:S(2)}, u32[]{:S(2)}) collective-permute-start(bf16[2,96,1152]{2,1,0:T(8,128)(2,1)} %get-tuple-element.80), channel_id=1, source_target_pairs={{0,2},{1,3},{2,0},{3,1},{4,6},{5,7},{6,4},{7,5},{8,10},{9,11},{10,... | collective-permute-start | bytes 1327112 | tf_op jit(solution)/shard_map/ppermute | solution.py:174
  145.1 33.0 %collective-permute-start.17 = (bf16[2,96,1152]{2,1,0:T(8,128)(2,1)}, bf16[2,96,1152]{2,1,0:T(8,128)(2,1)S(1)}, u32[]{:S(2)}, u32[]{:S(2)}) collective-permute-start(bf16[2,96,1152]{2,1,0:T(8,128)(2,1)} %get-tuple-element.90), channel_id=1, source_target_pairs={{0,4},{1,5},{2,6},{3,7},{4,0},{5,1},{6,2},{7,3},{8,12},{9,13},{10,... | collective-permute-start | bytes 1327112 | tf_op jit(solution)/shard_map/ppermute | solution.py:174
  149.3 38.0 %collective-permute-start.22 = (bf16[2,96,1152]{2,1,0:T(8,128)(2,1)}, bf16[2,96,1152]{2,1,0:T(8,128)(2,1)S(1)}, u32[]{:S(2)}, u32[]{:S(2)}) collective-permute-start(bf16[2,96,1152]{2,1,0:T(8,128)(2,1)} %get-tuple-element.95), channel_id=1, source_target_pairs={{0,5},{1,4},{2,7},{3,6},{4,1},{5,0},{6,3},{7,2},{8,13},{9,12},{10,... | collective-permute-start | bytes 1327112 | tf_op jit(solution)/shard_map/ppermute | solution.py:174
  149.6 39.8 %collective-permute-start.35 = (bf16[5,96,512]{2,1,0:T(8,128)(2,1)}, bf16[5,96,512]{2,1,0:T(8,128)(2,1)S(1)}, u32[]{:S(2)}, u32[]{:S(2)}) collective-permute-start(bf16[5,96,512]{2,1,0:T(8,128)(2,1)} %get-tuple-element.110), channel_id=1, source_target_pairs={{0,1},{1,0},{2,3},{3,2},{4,5},{5,4},{6,7},{7,6},{8,9},{9,8},{10,11... | collective-permute-start | bytes 1474568 | tf_op jit(solution)/shard_map/ppermute | solution.py:174
  149.9 37.8 %collective-permute-start.27 = (bf16[2,96,1152]{2,1,0:T(8,128)(2,1)}, bf16[2,96,1152]{2,1,0:T(8,128)(2,1)S(1)}, u32[]{:S(2)}, u32[]{:S(2)}) collective-permute-start(bf16[2,96,1152]{2,1,0:T(8,128)(2,1)} %get-tuple-element.100), channel_id=1, source_target_pairs={{0,6},{1,7},{2,4},{3,5},{4,2},{5,3},{6,0},{7,1},{8,14},{9,15},{10,... | collective-permute-start | bytes 1327112 | tf_op jit(solution)/shard_map/ppermute | solution.py:174
  151.4 36.5 %collective-permute-start.32 = (bf16[2,96,1152]{2,1,0:T(8,128)(2,1)S(1)}, bf16[2,96,1152]{2,1,0:T(8,128)(2,1)S(1)}, u32[]{:S(2)}, u32[]{:S(2)}) collective-permute-start(bf16[2,96,1152]{2,1,0:T(8,128)(2,1)S(1)} %copy-done.42), channel_id=1, source_target_pairs={{0,7},{1,6},{2,5},{3,4},{4,3},{5,2},{6,1},{7,0},{8,15},{9,14},{10,... | collective-permute-start | bytes 1327112 | tf_op jit(solution)/shard_map/ppermute | solution.py:174
  187.7 34.8 %collective-permute-start.38 = (bf16[5,96,512]{2,1,0:T(8,128)(2,1)}, bf16[5,96,512]{2,1,0:T(8,128)(2,1)S(1)}, u32[]{:S(2)}, u32[]{:S(2)}) collective-permute-start(bf16[5,96,512]{2,1,0:T(8,128)(2,1)} %get-tuple-element.113), channel_id=1, source_target_pairs={{0,4},{1,5},{2,6},{3,7},{4,0},{5,1},{6,2},{7,3},{8,12},{9,13},{10,... | collective-permute-start | bytes 1474568 | tf_op jit(solution)/shard_map/ppermute | solution.py:174
  187.9 44.3 %collective-permute-start.39 = (bf16[5,96,512]{2,1,0:T(8,128)(2,1)}, bf16[5,96,512]{2,1,0:T(8,128)(2,1)S(1)}, u32[]{:S(2)}, u32[]{:S(2)}) collective-permute-start(bf16[5,96,512]{2,1,0:T(8,128)(2,1)} %get-tuple-element.114), channel_id=1, source_target_pairs={{0,5},{1,4},{2,7},{3,6},{4,1},{5,0},{6,3},{7,2},{8,13},{9,12},{10,... | collective-permute-start | bytes 1474568 | tf_op jit(solution)/shard_map/ppermute | solution.py:174
  189.4 44.5 %collective-permute-start.40 = (bf16[5,96,512]{2,1,0:T(8,128)(2,1)}, bf16[5,96,512]{2,1,0:T(8,128)(2,1)S(1)}, u32[]{:S(2)}, u32[]{:S(2)}) collective-permute-start(bf16[5,96,512]{2,1,0:T(8,128)(2,1)} %get-tuple-element.115), channel_id=1, source_target_pairs={{0,6},{1,7},{2,4},{3,5},{4,2},{5,3},{6,0},{7,1},{8,14},{9,15},{10,... | collective-permute-start | bytes 1474568 | tf_op jit(solution)/shard_map/ppermute | solution.py:174
  192.1 42.3 %collective-permute-start.41 = (bf16[5,96,512]{2,1,0:T(8,128)(2,1)}, bf16[5,96,512]{2,1,0:T(8,128)(2,1)S(1)}, u32[]{:S(2)}, u32[]{:S(2)}) collective-permute-start(bf16[5,96,512]{2,1,0:T(8,128)(2,1)} %get-tuple-element.116), channel_id=1, source_target_pairs={{0,7},{1,6},{2,5},{3,4},{4,3},{5,2},{6,1},{7,0},{8,15},{9,14},{10,... | collective-permute-start | bytes 1474568 | tf_op jit(solution)/shard_map/ppermute | solution.py:174
  201.1 33.4 %collective-permute-start.42 = (bf16[5,96,512]{2,1,0:T(8,128)(2,1)}, bf16[5,96,512]{2,1,0:T(8,128)(2,1)S(1)}, u32[]{:S(2)}, u32[]{:S(2)}) collective-permute-start(bf16[5,96,512]{2,1,0:T(8,128)(2,1)} %get-tuple-element.118), channel_id=1, source_target_pairs={{0,1},{1,0},{2,3},{3,2},{4,5},{5,4},{6,7},{7,6},{8,9},{9,8},{10,11... | collective-permute-start | bytes 1474568 | tf_op jit(solution)/shard_map/ppermute | solution.py:174
  234.4 48.7 %collective-permute-start.3 = (bf16[3,96,1152]{2,1,0:T(8,128)(2,1)}, bf16[3,96,1152]{2,1,0:T(8,128)(2,1)S(1)}, u32[]{:S(2)}, u32[]{:S(2)}) collective-permute-start(bf16[3,96,1152]{2,1,0:T(8,128)(2,1)} %get-tuple-element.76), channel_id=1, source_target_pairs={{0,1},{1,0},{2,3},{3,2},{4,5},{5,4},{6,7},{7,6},{8,9},{9,8},{10,11... | collective-permute-start | bytes 1990664 | tf_op jit(solution)/shard_map/ppermute | solution.py:174
  234.5 49.8 %collective-permute-start.8 = (bf16[3,96,1152]{2,1,0:T(8,128)(2,1)}, bf16[3,96,1152]{2,1,0:T(8,128)(2,1)S(1)}, u32[]{:S(2)}, u32[]{:S(2)}) collective-permute-start(bf16[3,96,1152]{2,1,0:T(8,128)(2,1)} %get-tuple-element.81), channel_id=1, source_target_pairs={{0,2},{1,3},{2,0},{3,1},{4,6},{5,7},{6,4},{7,5},{8,10},{9,11},{10,... | collective-permute-start | bytes 1990664 | tf_op jit(solution)/shard_map/ppermute | solution.py:174
  256.9 38.5 %collective-permute-start.13 = (bf16[3,96,1152]{2,1,0:T(8,128)(2,1)}, bf16[3,96,1152]{2,1,0:T(8,128)(2,1)S(1)}, u32[]{:S(2)}, u32[]{:S(2)}) collective-permute-start(bf16[3,96,1152]{2,1,0:T(8,128)(2,1)} %get-tuple-element.86), channel_id=1, source_target_pairs={{0,3},{1,2},{2,1},{3,0},{4,7},{5,6},{6,5},{7,4},{8,11},{9,10},{10,... | collective-permute-start | bytes 1990664 | tf_op jit(solution)/shard_map/ppermute | solution.py:174
  281.1 56.7 %collective-permute-start.23 = (bf16[3,96,1152]{2,1,0:T(8,128)(2,1)}, bf16[3,96,1152]{2,1,0:T(8,128)(2,1)S(1)}, u32[]{:S(2)}, u32[]{:S(2)}) collective-permute-start(bf16[3,96,1152]{2,1,0:T(8,128)(2,1)} %get-tuple-element.96), channel_id=1, source_target_pairs={{0,5},{1,4},{2,7},{3,6},{4,1},{5,0},{6,3},{7,2},{8,13},{9,12},{10,... | collective-permute-start | bytes 1990664 | tf_op jit(solution)/shard_map/ppermute | solution.py:174
  283.2 56.1 %collective-permute-start.28 = (bf16[3,96,1152]{2,1,0:T(8,128)(2,1)}, bf16[3,96,1152]{2,1,0:T(8,128)(2,1)}, u32[]{:S(2)}, u32[]{:S(2)}) collective-permute-start(bf16[3,96,1152]{2,1,0:T(8,128)(2,1)} %get-tuple-element.101), channel_id=1, source_target_pairs={{0,6},{1,7},{2,4},{3,5},{4,2},{5,3},{6,0},{7,1},{8,14},{9,15},{10,... | collective-permute-start | bytes 1990664 | tf_op jit(solution)/shard_map/ppermute | solution.py:174
  284.3 56.4 %collective-permute-start.33 = (bf16[3,96,1152]{2,1,0:T(8,128)(2,1)}, bf16[3,96,1152]{2,1,0:T(8,128)(2,1)}, u32[]{:S(2)}, u32[]{:S(2)}) collective-permute-start(bf16[3,96,1152]{2,1,0:T(8,128)(2,1)} %get-tuple-element.106), channel_id=1, source_target_pairs={{0,7},{1,6},{2,5},{3,4},{4,3},{5,2},{6,1},{7,0},{8,15},{9,14},{10,... | collective-permute-start | bytes 1990664 | tf_op jit(solution)/shard_map/ppermute | solution.py:174
  295.3 78.2 %collective-permute-start.14 = (bf16[5,96,128]{2,1,0:T(8,128)(2,1)}, bf16[5,96,128]{2,1,0:T(8,128)(2,1)}, u32[]{:S(2)}, u32[]{:S(2)}) collective-permute-start(bf16[5,96,128]{2,1,0:T(8,128)(2,1)} %get-tuple-element.87), channel_id=1, source_target_pairs={{0,3},{1,2},{2,1},{3,0},{4,7},{5,6},{6,5},{7,4},{8,11},{9,10},{10,... | collective-permute-start | bytes 368648 | tf_op jit(solution)/shard_map/ppermute | solution.py:174
  297.5 76.0 %collective-permute-start.19 = (bf16[5,96,128]{2,1,0:T(8,128)(2,1)}, bf16[5,96,128]{2,1,0:T(8,128)(2,1)}, u32[]{:S(2)}, u32[]{:S(2)}) collective-permute-start(bf16[5,96,128]{2,1,0:T(8,128)(2,1)} %get-tuple-element.92), channel_id=1, source_target_pairs={{0,4},{1,5},{2,6},{3,7},{4,0},{5,1},{6,2},{7,3},{8,12},{9,13},{10,... | collective-permute-start | bytes 368648 | tf_op jit(solution)/shard_map/ppermute | solution.py:174
  337.9 35.7 %collective-permute-start.24 = (bf16[5,96,128]{2,1,0:T(8,128)(2,1)}, bf16[5,96,128]{2,1,0:T(8,128)(2,1)}, u32[]{:S(2)}, u32[]{:S(2)}) collective-permute-start(bf16[5,96,128]{2,1,0:T(8,128)(2,1)} %get-tuple-element.97), channel_id=1, source_target_pairs={{0,5},{1,4},{2,7},{3,6},{4,1},{5,0},{6,3},{7,2},{8,13},{9,12},{10,... | collective-permute-start | bytes 368648 | tf_op jit(solution)/shard_map/ppermute | solution.py:174
  339.3 34.3 %collective-permute-start.29 = (bf16[5,96,128]{2,1,0:T(8,128)(2,1)}, bf16[5,96,128]{2,1,0:T(8,128)(2,1)}, u32[]{:S(2)}, u32[]{:S(2)}) collective-permute-start(bf16[5,96,128]{2,1,0:T(8,128)(2,1)} %get-tuple-element.102), channel_id=1, source_target_pairs={{0,6},{1,7},{2,4},{3,5},{4,2},{5,3},{6,0},{7,1},{8,14},{9,15},{10,... | collective-permute-start | bytes 368648 | tf_op jit(solution)/shard_map/ppermute | solution.py:174
  (75 other events, 5212.6 us)
where the time goes:
time: 381 us; the launch traced here: 380 us
  waiting for transfers between devices  203 us (53%)
  Pallas kernels  122 us (32%)
  starting transfers between devices  52.6 us (14%)
    ppermute x49, waiting for transfers between devices, transform(): block = lax.ppermute(block, 'dev', [(i, i ^ k) for i in range(n_dev)])  203 us
    pallas_call x4, Pallas kernels, transform(): pl.pallas_call(functools.partial(send_kernel, n, n_dev, rows, tiles, last...  75.6 us
    ppermute x49, starting transfers between devices, transform(): block = lax.ppermute(block, 'dev', [(i, i ^ k) for i in range(n_dev)])  52.6 us
    pallas_call x3, Pallas kernels, transform(): pl.pallas_call(functools.partial(out_kernel, n, n_in, w, depth, pack), gr...  38.1 us
    pallas_call x1, Pallas kernels, transform(): pl.pallas_call(functools.partial(first_kernel, n, n_dev, tiles), grid=(1,...  8.8 us
  transfers between devices with their start and end apart: 49, of which 20 were waited for; matrix products, arithmetic and copies ran while one was open for 0% of the time, Pallas kernels for 8%

commit v1 on v0

--- a/solution.py
+++ b/solution.py
@@ -8,8 +8,8 @@
 from jax.sharding import PartitionSpec as P
 
 
-PIECES = ((0, 1, (1152,)), (1, 1, (1152,)), (2, 2, (1152,)), (4, 3, (1152,)), (7, 5, (512, 512, 128)))
-TILES = ((0, 512, 32, 1), (512, 512, 32, 1), (1024, 128, 32, 2))
+PIECES = ((0, 2, (96,)), (2, 4, (96,)), (6, 6, (40, 32, 16, 8)))
+TILES = ((0, 40), (40, 32), (72, 16), (88, 8))
 F32, BF16 = jnp.float32, jnp.bfloat16
 
 
@@ -57,7 +57,7 @@
     l4_ref[...] = jnp.where(keep, wide, 0.0).astype(BF16)
 
 
-def one_row(n, n_dev, tiles, me, a_ref, l1_ref, r2_ref, ct_ref, outs, t1_ref):
+def one_row(n, n_dev, tiles, me, a_ref, l1_ref, r2_ref, ct_ref, outs, t1_ref, row):
     nj = n // n_dev
     zero = jnp.zeros((8 * n, 128 - n), BF16)
 
@@ -80,45 +80,38 @@
         g = dot(ct_ref[...], h).astype(BF16)
         off = 0
         for t_i, w in enumerate(tiles):
-            outs[k * len(tiles) + t_i][0] = g[:, off:off + w]
+            outs[k * len(tiles) + t_i][row] = g[off:off + w]
             off += w
 
 
-def first_kernel(n, n_dev, tiles, me_ref, a_hbm, c_ref, l1_ref, r2_ref, ct_ref, *rest):
+def first_kernel(n, n_dev, count, tiles, me_ref, a_hbm, c_ref, l1_ref, r2_ref, ct_ref, *rest):
     outs, (a_buf, t1_ref, sem) = rest[:-3], rest[-3:]
-    copy = pltpu.make_async_copy(a_hbm.at[0], a_buf, sem)
-    copy.start()
+    copies = [pltpu.make_async_copy(a_hbm.at[i], a_buf.at[i], sem.at[i]) for i in range(count)]
+    for copy in copies:
+        copy.start()
     build_first(n, c_ref, l1_ref, r2_ref, ct_ref)
-    copy.wait()
-    one_row(n, n_dev, tiles, me_ref[0], a_buf, l1_ref, r2_ref, ct_ref, outs, t1_ref)
+
+    def row(i, carry):
+        pltpu.make_async_copy(a_hbm.at[i], a_buf.at[i], sem.at[i]).wait()
+        one_row(n, n_dev, tiles, me_ref[0], a_buf.at[i], l1_ref, r2_ref, ct_ref, outs, t1_ref, i)
+        return carry
+
+    lax.fori_loop(0, count, row, 0)
 
 
 def send_kernel(n, n_dev, rows, tiles, last, me_ref, a_ref, l1_ref, r2_ref, ct_ref, before, *rest):
     outs, t1_ref = rest[:n_dev * len(tiles)], rest[-1]
-    one_row(n, n_dev, tiles, me_ref[0], a_ref.at[0], l1_ref, r2_ref, ct_ref, outs, t1_ref)
+    one_row(n, n_dev, tiles, me_ref[0], a_ref.at[0], l1_ref, r2_ref, ct_ref, outs, t1_ref, 0)
     if last:
         @pl.when(pl.program_id(0) == 0)
         def _():
             build_last(n, rows, me_ref[0], ct_ref, rest[-2])
 
 
-def out_kernel(n, n_in, width, depth, pack, *refs):
+def out_kernel(n, n_in, wide, *refs):
     l4_ref, out_ref = refs[n_in], refs[-1]
-    ins = refs[:n_in]
-
-    def step(s, carry):
-        a0 = pl.multiple_of(s * 8 * pack, 8 * pack)
-        cols = []
-        for x in range(pack):
-            cols.append(jnp.concatenate(
-                [r[:, pl.ds(a0 + 8 * x, 8), :].reshape(-1, width) for r in ins], axis=0))
-        rhs = cols[0] if pack == 1 else jnp.concatenate(cols, axis=1)
-        v = dot(l4_ref[...], rhs)
-        for x in range(pack):
-            out_ref[:, pl.ds(a0 + 8 * x, 8), :] = v[:, x * width:(x + 1) * width].reshape(n, 8, width)
-        return carry
-
-    lax.fori_loop(0, depth // (8 * pack), step, 0)
+    rhs = jnp.concatenate([r[...].reshape(-1, wide) for r in refs[:n_in]], axis=0)
+    out_ref[...] = dot(l4_ref[...], rhs).reshape(n, 8, wide)
 
 
 def solution(mesh):
@@ -139,17 +132,17 @@
         square, second = (8 * n, 8 * n), (512, 4 * n)
         got = [[] for _ in range(n_dev)]
         for i, (p0, count, tiles) in enumerate(PIECES):
-            block_specs = [pl.BlockSpec((1, n, w), lambda i: (i, 0, 0)) for _ in range(n_dev) for w in tiles]
-            block_shapes = [jax.ShapeDtypeStruct((count, n, w), BF16) for _ in range(n_dev) for w in tiles]
+            block_specs = [pl.BlockSpec((count if i == 0 else 1, w, wide), lambda i: (i, 0, 0)) for _ in range(n_dev) for w in tiles]
+            block_shapes = [jax.ShapeDtypeStruct((count, w, wide), BF16) for _ in range(n_dev) for w in tiles]
             t1 = pltpu.VMEM((n, n, 128), BF16)
             if i == 0:
                 l1, r2, ct, *sent = pl.pallas_call(
-                    functools.partial(first_kernel, n, n_dev, tiles),
+                    functools.partial(first_kernel, n, n_dev, count, tiles),
                     grid=(1,),
                     in_specs=[smem, hbm, vmem],
                     out_specs=[const(square), const(second), const((n, n))] + block_specs,
                     out_shape=[jax.ShapeDtypeStruct(s, BF16) for s in (square, second, (n, n))] + block_shapes,
-                    scratch_shapes=[pltpu.VMEM((n, n, n), BF16), t1, pltpu.SemaphoreType.DMA],
+                    scratch_shapes=[pltpu.VMEM((count, n, n, n), BF16), t1, pltpu.SemaphoreType.DMA((count,))],
                     name='first',
                 )(me_arr, ao_rows, coeffs)
             else:
@@ -175,14 +168,14 @@
                     got[k].append((block, t_i if len(tiles) > 1 else None))
 
         out = None
-        for t_i, (off, w, depth, pack) in enumerate(TILES):
+        for t_i, (a0, size) in enumerate(TILES):
             ins, specs = [], []
             for k in range(n_dev):
                 for block, tile in got[k]:
                     if tile in (None, t_i):
-                        lane = off // w if tile is None else 0
+                        base = a0 // 8 if tile is None else 0
                         ins.append(block)
-                        specs.append(pl.BlockSpec((block.shape[0], depth, w), lambda i, lane=lane: (0, i, lane)))
+                        specs.append(pl.BlockSpec((block.shape[0], 8, wide), lambda i, base=base: (0, base + i, 0)))
             n_in = len(ins)
             ins.append(l4)
             specs.append(const(square))
@@ -190,10 +183,10 @@
                 ins.append(out)
                 specs.append(hbm)
             out = pl.pallas_call(
-                functools.partial(out_kernel, n, n_in, w, depth, pack),
-                grid=(n // depth,),
+                functools.partial(out_kernel, n, n_in, wide),
+                grid=(size // 8,),
                 in_specs=specs,
-                out_specs=pl.BlockSpec((n, depth, w), lambda i, off=off, w=w: (0, i, off // w)),
+                out_specs=pl.BlockSpec((n, 8, wide), lambda i, a0=a0: (0, a0 // 8 + i, 0)),
                 out_shape=jax.ShapeDtypeStruct((n, n, wide), F32),
                 input_output_aliases={} if t_i == 0 else {len(ins) - 1: 0},
                 name='out',

time: 381 us -> 378 us (level)
  starting transfers between devices: 52.6 us -> 46.4 us
    pallas_call x4 -> x2, Pallas kernels: 75.6 us -> 65.4 us  [transform(): pl.pallas_call(functools.partial(send_kernel, n, n_dev, rows, tiles, last...]
    pallas_call x4 -> x5, Pallas kernels: 46.9 us -> 55.3 us  [the longest x4 40.1 us: transform(): pl.pallas_call(functools.partial(out_kernel, n, n_in, wide), grid=(size /...]
    ppermute x49 -> x42, starting transfers between devices: 52.6 us -> 46.4 us  [transform(): block = lax.ppermute(block, 'dev', [(i, i ^ k) for i in range(n_dev)])]
    ppermute x49 -> x42, waiting for transfers between devices: 203 us -> 205 us  [transform(): block = lax.ppermute(block, 'dev', [(i, i ^ k) for i in range(n_dev)])]
  transfers between devices with their start and end apart: 49 -> 42, of which waited for: 20 -> 17; matrix products, arithmetic and copies ran while one was open for 0% -> 0% of each run, Pallas kernels for 8% -> 9%
where the time goes in v1:
time: 378 us; the launch traced here: 377 us
  waiting for transfers between devices  205 us (54%)
  Pallas kernels  121 us (32%)
  starting transfers between devices  46.4 us (12%)
  local copies, waits for them, and re-layouts  4.34 us (1%)
    ppermute x42, waiting for transfers between devices, transform(): block = lax.ppermute(block, 'dev', [(i, i ^ k) for i in range(n_dev)])  205 us
    pallas_call x2, Pallas kernels, transform(): pl.pallas_call(functools.partial(send_kernel, n, n_dev, rows, tiles, last...  65.4 us
    ppermute x42, starting transfers between devices, transform(): block = lax.ppermute(block, 'dev', [(i, i ^ k) for i in range(n_dev)])  46.4 us
    pallas_call x4, Pallas kernels, transform(): pl.pallas_call(functools.partial(out_kernel, n, n_in, wide), grid=(size /...  40.1 us
    pallas_call x1, Pallas kernels, transform(): pl.pallas_call(functools.partial(first_kernel, n, n_dev, count, tiles), g...  15.2 us
  transfers between devices with their start and end apart: 42, of which 17 were waited for; matrix products, arithmetic and copies ran while one was open for 0% of the time, Pallas kernels for 9%

profile of v1, /device:TPU:0, one launch (start us, length us, event | category | flops | bytes accessed | tf_op | source)
XLA Modules:
  0.0 377.1 jit_solution(8500909048747956430)
XLA Ops:
  0.0 15.2 %first.1 = (bf16[768,768]{1,0:T(8,128)(2,1)}, bf16[512,384]{1,0:T(8,128)(2,1)}, bf16[96,96]{1,0:T(8,128)(2,1)}, bf16[2,96,1152]{2,1,0:T(8,128)(2,1)}, bf16[2,96,...) custom-call(s32[1]{0:T(128)} %bitcast.me_ref, ...), custom_call_target="tpu_custom_call" | custom-call | tf_op jit(solution)/shard_map/first/pallas_call | solution.py:139
  15.3 27.6 %send.2 = (bf16[4,96,1152]{2,1,0:T(8,128)(2,1)}, bf16[4,96,1152]{2,1,0:T(8,128)(2,1)}, bf16[4,96,1152]{2,1,0:T(8,128)(2,1)}, bf16[4,96,1152]{2,1,0:T(8,128)(2,1)...) custom-call(s32[1]{0:T(128)} %bitcast.me_ref, ...), custom_call_target="tpu_custom_call" | custom-call | tf_op jit(solution)/shard_map/send/pallas_call | solution.py:150
  42.9 37.9 %send.3 = (bf16[6,40,1152]{2,1,0:T(8,128)(2,1)}, bf16[6,32,1152]{2,1,0:T(8,128)(2,1)}, bf16[6,16,1152]{2,1,0:T(8,128)(2,1)}, bf16[6,8,1152]{2,1,0:T(8,128)(2,1)}...) custom-call(s32[1]{0:T(128)} %bitcast.me_ref, ...), custom_call_target="tpu_custom_call" | custom-call | tf_op jit(solution)/shard_map/send/pallas_call | solution.py:150
  81.5 2.5 collective-permute-start.5
  88.9 2.3 collective-permute-start.26
  93.6 3.7 collective-permute-done.23.refs_11_
  105.8 20.7 %collective-permute-done.27.refs_23_ = bf16[6,16,1152]{2,1,0:T(8,128)(2,1)S(1)} collective-permute-done((bf16[6,16,1152]{2,1,0:T(8,128)(2,1)}, bf16[6,16,1152]{2,1,0:T(8,128)(2,1)S(1)}, u32[]{:S(2)}, u32[]{:S(2)}) %collective-permute-start.27) | collective-permute-done | bytes 221216 | tf_op jit(solution)/shard_map/ppermute | solution.py:167
  127.5 2.6 collective-permute-start.15
  132.3 25.8 %collective-permute-done.12.refs_15_ = bf16[2,96,1152]{2,1,0:T(8,128)(2,1)S(1)} collective-permute-done((bf16[2,96,1152]{2,1,0:T(8,128)(2,1)S(1)}, bf16[2,96,1152]{2,1,0:T(8,128)(2,1)S(1)}, u32[]{:S(2)}, u32[]{:S(2)}) %collective-permute-start.12) | collective-permute-done | bytes 442400 | tf_op jit(solution)/shard_map/ppermute | solution.py:167
  163.6 7.2 %collective-permute-done.30.refs_11_ = bf16[6,32,1152]{2,1,0:T(8,128)(2,1)S(1)} collective-permute-done((bf16[6,32,1152]{2,1,0:T(8,128)(2,1)}, bf16[6,32,1152]{2,1,0:T(8,128)(2,1)S(1)}, u32[]{:S(2)}, u32[]{:S(2)}) %collective-permute-start.30) | collective-permute-done | bytes 442400 | tf_op jit(solution)/shard_map/ppermute | solution.py:167
  172.8 19.3 %collective-permute-done.31.refs_14_ = bf16[6,32,1152]{2,1,0:T(8,128)(2,1)S(1)} collective-permute-done((bf16[6,32,1152]{2,1,0:T(8,128)(2,1)}, bf16[6,32,1152]{2,1,0:T(8,128)(2,1)S(1)}, u32[]{:S(2)}, u32[]{:S(2)}) %collective-permute-start.31) | collective-permute-done | bytes 442400 | tf_op jit(solution)/shard_map/ppermute | solution.py:167
  192.6 6.8 %collective-permute-done.32.refs_17_ = bf16[6,32,1152]{2,1,0:T(8,128)(2,1)S(1)} collective-permute-done((bf16[6,32,1152]{2,1,0:T(8,128)(2,1)}, bf16[6,32,1152]{2,1,0:T(8,128)(2,1)S(1)}, u32[]{:S(2)}, u32[]{:S(2)}) %collective-permute-start.32) | collective-permute-done | bytes 442400 | tf_op jit(solution)/shard_map/ppermute | solution.py:167
  204.2 9.8 %collective-permute-done.37.refs_11_ = bf16[6,40,1152]{2,1,0:T(8,128)(2,1)S(1)} collective-permute-done((bf16[6,40,1152]{2,1,0:T(8,128)(2,1)}, bf16[6,40,1152]{2,1,0:T(8,128)(2,1)S(1)}, u32[]{:S(2)}, u32[]{:S(2)}) %collective-permute-start.37) | collective-permute-done | bytes 552992 | tf_op jit(solution)/shard_map/ppermute | solution.py:167
  218.2 9.3 %collective-permute-done.39.refs_17_ = bf16[6,40,1152]{2,1,0:T(8,128)(2,1)S(1)} collective-permute-done((bf16[6,40,1152]{2,1,0:T(8,128)(2,1)}, bf16[6,40,1152]{2,1,0:T(8,128)(2,1)S(1)}, u32[]{:S(2)}, u32[]{:S(2)}) %collective-permute-start.39) | collective-permute-done | bytes 552992 | tf_op jit(solution)/shard_map/ppermute | solution.py:167
  228.2 18.4 %collective-permute-done.40.refs_20_ = bf16[6,40,1152]{2,1,0:T(8,128)(2,1)S(1)} collective-permute-done((bf16[6,40,1152]{2,1,0:T(8,128)(2,1)}, bf16[6,40,1152]{2,1,0:T(8,128)(2,1)S(1)}, u32[]{:S(2)}, u32[]{:S(2)}) %collective-permute-start.40) | collective-permute-done | bytes 552992 | tf_op jit(solution)/shard_map/ppermute | solution.py:167
  248.1 8.6 %collective-permute-done.41.refs_23_ = bf16[6,40,1152]{2,1,0:T(8,128)(2,1)S(1)} collective-permute-done((bf16[6,40,1152]{2,1,0:T(8,128)(2,1)}, bf16[6,40,1152]{2,1,0:T(8,128)(2,1)S(1)}, u32[]{:S(2)}, u32[]{:S(2)}) %collective-permute-start.41) | collective-permute-done | bytes 552992 | tf_op jit(solution)/shard_map/ppermute | solution.py:167
  256.7 2.7 collective-permute-start.13
  260.6 15.0 %collective-permute-done.7.refs_10_ = bf16[4,96,1152]{2,1,0:T(8,128)(2,1)S(1)} collective-permute-done((bf16[4,96,1152]{2,1,0:T(8,128)(2,1)}, bf16[4,96,1152]{2,1,0:T(8,128)(2,1)S(1)}, u32[]{:S(2)}, u32[]{:S(2)}) %collective-permute-start.7) | collective-permute-done | bytes 884768 | tf_op jit(solution)/shard_map/ppermute | solution.py:167
  275.7 2.2 collective-permute-start.8
  279.1 54.1 %collective-permute-done.13.refs_16_ = bf16[4,96,1152]{2,1,0:T(8,128)(2,1)} collective-permute-done((bf16[4,96,1152]{2,1,0:T(8,128)(2,1)}, bf16[4,96,1152]{2,1,0:T(8,128)(2,1)}, u32[]{:S(2)}, u32[]{:S(2)}) %collective-permute-start.13) | collective-permute-done | bytes 884768 | tf_op jit(solution)/shard_map/ppermute | solution.py:167
  336.9 15.2 %out.4.refs_25_ = f32[96,96,1152]{2,1,0:T(8,128)} custom-call(bf16[2,96,1152]{2,1,0:T(8,128)(2,1)} %get-tuple-element.57.before.refs_0_, bf16[4,96,1152]{2,1,0:T(8,128)(2,1)} %get-tuple-element.61.before.refs_1_, bf16[6,40,1152]{2,1,0:T(8,128)(2,1)} %get-tuple-element.101.refs_2_, bf16[2,96,1152]{2,1,0:T(8,128)(2,1)} %copy-done.4, ...), custom_call_target="tpu_custom_call" | custom-call | tf_op jit(solution)/shard_map/out/pallas_call | solution.py:185
  352.1 12.2 %out.5.refs_25_ = f32[96,96,1152]{2,1,0:T(8,128)} custom-call(bf16[2,96,1152]{2,1,0:T(8,128)(2,1)} %get-tuple-element.57.before.refs_0_, bf16[4,96,1152]{2,1,0:T(8,128)(2,1)} %get-tuple-element.61.before.refs_1_, bf16[6,32,1152]{2,1,0:T(8,128)(2,1)} %get-tuple-element.93.refs_2_, bf16[2,96,1152]{2,1,0:T(8,128)(2,1)} %copy-done.4, ...), custom_call_target="tpu_custom_call", output_to_operand_aliasing={{}: (25, {})} | custom-call | tf_op jit(solution)/shard_map/out/pallas_call | solution.py:185
  364.3 7.3 %out.6.refs_25_ = f32[96,96,1152]{2,1,0:T(8,128)} custom-call(bf16[2,96,1152]{2,1,0:T(8,128)(2,1)} %get-tuple-element.57.before.refs_0_, bf16[4,96,1152]{2,1,0:T(8,128)(2,1)} %get-tuple-element.61.before.refs_1_, bf16[6,16,1152]{2,1,0:T(8,128)(2,1)} %get-tuple-element.85.refs_2_, bf16[2,96,1152]{2,1,0:T(8,128)(2,1)} %copy-done.4, ...), custom_call_target="tpu_custom_call", output_to_operand_aliasing={{}: (25, {})} | custom-call | tf_op jit(solution)/shard_map/out/pallas_call | solution.py:185
  371.7 5.5 %out.7 = f32[96,96,1152]{2,1,0:T(8,128)} custom-call(bf16[2,96,1152]{2,1,0:T(8,128)(2,1)} %get-tuple-element.57.before.refs_0_, bf16[4,96,1152]{2,1,0:T(8,128)(2,1)} %get-tuple-element.61.before.refs_1_, bf16[6,8,1152]{2,1,0:T(8,128)(2,1)} %get-tuple-element.62.refs_2_, bf16[2,96,1152]{2,1,0:T(8,128)(2,1)} %copy-done.4, ...), custom_call_target="tpu_custom_call", output_to_operand_aliasing={{}: (25, {})} | custom-call | tf_op jit(solution)/shard_map/out/pallas_call | solution.py:185
  (149 shorter events, 45.0 us)
Async XLA Ops:
  93.6 33.9 %collective-permute-start = (bf16[2,96,1152]{2,1,0:T(8,128)(2,1)S(1)}, bf16[2,96,1152]{2,1,0:T(8,128)(2,1)S(1)}, u32[]{:S(2)}, u32[]{:S(2)}) collective-permute-start(bf16[2,96,1152]{2,1,0:T(8,128)(2,1)S(1)} %copy-done.40), channel_id=1, source_target_pairs={{0,1},{1,0},{2,3},{3,2},{4,5},{5,4},{6,7},{7,6},{8,9},{9,8},{10,11... | collective-permute-start | bytes 1327112 | tf_op jit(solution)/shard_map/ppermute | solution.py:167
  98.0 32.2 %collective-permute-start.3 = (bf16[2,96,1152]{2,1,0:T(8,128)(2,1)S(1)}, bf16[2,96,1152]{2,1,0:T(8,128)(2,1)S(1)}, u32[]{:S(2)}, u32[]{:S(2)}) collective-permute-start(bf16[2,96,1152]{2,1,0:T(8,128)(2,1)S(1)} %copy-done.39), channel_id=1, source_target_pairs={{0,2},{1,3},{2,0},{3,1},{4,6},{5,7},{6,4},{7,5},{8,10},{9,11},{10,... | collective-permute-start | bytes 1327112 | tf_op jit(solution)/shard_map/ppermute | solution.py:167
  127.2 30.9 %collective-permute-start.12 = (bf16[2,96,1152]{2,1,0:T(8,128)(2,1)S(1)}, bf16[2,96,1152]{2,1,0:T(8,128)(2,1)S(1)}, u32[]{:S(2)}, u32[]{:S(2)}) collective-permute-start(bf16[2,96,1152]{2,1,0:T(8,128)(2,1)S(1)} %copy-done.36), channel_id=1, source_target_pairs={{0,5},{1,4},{2,7},{3,6},{4,1},{5,0},{6,3},{7,2},{8,13},{9,12},{10,... | collective-permute-start | bytes 1327112 | tf_op jit(solution)/shard_map/ppermute | solution.py:167
  127.5 32.3 %collective-permute-start.15 = (bf16[2,96,1152]{2,1,0:T(8,128)(2,1)S(1)}, bf16[2,96,1152]{2,1,0:T(8,128)(2,1)S(1)}, u32[]{:S(2)}, u32[]{:S(2)}) collective-permute-start(bf16[2,96,1152]{2,1,0:T(8,128)(2,1)S(1)} %copy-done.35), channel_id=1, source_target_pairs={{0,6},{1,7},{2,4},{3,5},{4,2},{5,3},{6,0},{7,1},{8,14},{9,15},{10,... | collective-permute-start | bytes 1327112 | tf_op jit(solution)/shard_map/ppermute | solution.py:167
  130.2 30.9 %collective-permute-start.28 = (bf16[6,32,1152]{2,1,0:T(8,128)(2,1)}, bf16[6,32,1152]{2,1,0:T(8,128)(2,1)S(1)}, u32[]{:S(2)}, u32[]{:S(2)}) collective-permute-start(bf16[6,32,1152]{2,1,0:T(8,128)(2,1)} %get-tuple-element.94), channel_id=1, source_target_pairs={{0,1},{1,0},{2,3},{3,2},{4,5},{5,4},{6,7},{7,6},{8,9},{9,8},{10,11... | collective-permute-start | bytes 1327112 | tf_op jit(solution)/shard_map/ppermute | solution.py:167
  130.7 31.3 %collective-permute-start.29 = (bf16[6,32,1152]{2,1,0:T(8,128)(2,1)}, bf16[6,32,1152]{2,1,0:T(8,128)(2,1)S(1)}, u32[]{:S(2)}, u32[]{:S(2)}) collective-permute-start(bf16[6,32,1152]{2,1,0:T(8,128)(2,1)} %get-tuple-element.95), channel_id=1, source_target_pairs={{0,2},{1,3},{2,0},{3,1},{4,6},{5,7},{6,4},{7,5},{8,10},{9,11},{10,... | collective-permute-start | bytes 1327112 | tf_op jit(solution)/shard_map/ppermute | solution.py:167
  159.9 32.2 %collective-permute-start.31 = (bf16[6,32,1152]{2,1,0:T(8,128)(2,1)}, bf16[6,32,1152]{2,1,0:T(8,128)(2,1)S(1)}, u32[]{:S(2)}, u32[]{:S(2)}) collective-permute-start(bf16[6,32,1152]{2,1,0:T(8,128)(2,1)} %get-tuple-element.97), channel_id=1, source_target_pairs={{0,4},{1,5},{2,6},{3,7},{4,0},{5,1},{6,2},{7,3},{8,12},{9,13},{10,... | collective-permute-start | bytes 1327112 | tf_op jit(solution)/shard_map/ppermute | solution.py:167
  160.4 39.0 %collective-permute-start.32 = (bf16[6,32,1152]{2,1,0:T(8,128)(2,1)}, bf16[6,32,1152]{2,1,0:T(8,128)(2,1)S(1)}, u32[]{:S(2)}, u32[]{:S(2)}) collective-permute-start(bf16[6,32,1152]{2,1,0:T(8,128)(2,1)} %get-tuple-element.98), channel_id=1, source_target_pairs={{0,5},{1,4},{2,7},{3,6},{4,1},{5,0},{6,3},{7,2},{8,13},{9,12},{10,... | collective-permute-start | bytes 1327112 | tf_op jit(solution)/shard_map/ppermute | solution.py:167
  161.1 39.6 %collective-permute-start.33 = (bf16[6,32,1152]{2,1,0:T(8,128)(2,1)}, bf16[6,32,1152]{2,1,0:T(8,128)(2,1)S(1)}, u32[]{:S(2)}, u32[]{:S(2)}) collective-permute-start(bf16[6,32,1152]{2,1,0:T(8,128)(2,1)} %get-tuple-element.99), channel_id=1, source_target_pairs={{0,6},{1,7},{2,4},{3,5},{4,2},{5,3},{6,0},{7,1},{8,14},{9,15},{10,... | collective-permute-start | bytes 1327112 | tf_op jit(solution)/shard_map/ppermute | solution.py:167
  162.7 38.9 %collective-permute-start.35 = (bf16[6,40,1152]{2,1,0:T(8,128)(2,1)}, bf16[6,40,1152]{2,1,0:T(8,128)(2,1)S(1)}, u32[]{:S(2)}, u32[]{:S(2)}) collective-permute-start(bf16[6,40,1152]{2,1,0:T(8,128)(2,1)} %get-tuple-element.102), channel_id=1, source_target_pairs={{0,1},{1,0},{2,3},{3,2},{4,5},{5,4},{6,7},{7,6},{8,9},{9,8},{10,11... | collective-permute-start | bytes 1658888 | tf_op jit(solution)/shard_map/ppermute | solution.py:167
  201.6 57.8 %collective-permute-start.1 = (bf16[4,96,1152]{2,1,0:T(8,128)(2,1)}, bf16[4,96,1152]{2,1,0:T(8,128)(2,1)S(1)}, u32[]{:S(2)}, u32[]{:S(2)}) collective-permute-start(bf16[4,96,1152]{2,1,0:T(8,128)(2,1)} %get-tuple-element.64), channel_id=1, source_target_pairs={{0,1},{1,0},{2,3},{3,2},{4,5},{5,4},{6,7},{7,6},{8,9},{9,8},{10,11... | collective-permute-start | bytes 2654216 | tf_op jit(solution)/shard_map/ppermute | solution.py:167
  201.7 58.5 %collective-permute-start.4 = (bf16[4,96,1152]{2,1,0:T(8,128)(2,1)}, bf16[4,96,1152]{2,1,0:T(8,128)(2,1)S(1)}, u32[]{:S(2)}, u32[]{:S(2)}) collective-permute-start(bf16[4,96,1152]{2,1,0:T(8,128)(2,1)} %get-tuple-element.67), channel_id=1, source_target_pairs={{0,2},{1,3},{2,0},{3,1},{4,6},{5,7},{6,4},{7,5},{8,10},{9,11},{10,... | collective-permute-start | bytes 2654216 | tf_op jit(solution)/shard_map/ppermute | solution.py:167
  214.0 32.6 %collective-permute-start.40 = (bf16[6,40,1152]{2,1,0:T(8,128)(2,1)}, bf16[6,40,1152]{2,1,0:T(8,128)(2,1)S(1)}, u32[]{:S(2)}, u32[]{:S(2)}) collective-permute-start(bf16[6,40,1152]{2,1,0:T(8,128)(2,1)} %get-tuple-element.107), channel_id=1, source_target_pairs={{0,6},{1,7},{2,4},{3,5},{4,2},{5,3},{6,0},{7,1},{8,14},{9,15},{10,... | collective-permute-start | bytes 1658888 | tf_op jit(solution)/shard_map/ppermute | solution.py:167
  216.4 40.3 %collective-permute-start.41 = (bf16[6,40,1152]{2,1,0:T(8,128)(2,1)}, bf16[6,40,1152]{2,1,0:T(8,128)(2,1)S(1)}, u32[]{:S(2)}, u32[]{:S(2)}) collective-permute-start(bf16[6,40,1152]{2,1,0:T(8,128)(2,1)} %get-tuple-element.108), channel_id=1, source_target_pairs={{0,7},{1,6},{2,5},{3,4},{4,3},{5,2},{6,1},{7,0},{8,15},{9,14},{10,... | collective-permute-start | bytes 1658888 | tf_op jit(solution)/shard_map/ppermute | solution.py:167
  227.5 48.1 %collective-permute-start.7 = (bf16[4,96,1152]{2,1,0:T(8,128)(2,1)}, bf16[4,96,1152]{2,1,0:T(8,128)(2,1)S(1)}, u32[]{:S(2)}, u32[]{:S(2)}) collective-permute-start(bf16[4,96,1152]{2,1,0:T(8,128)(2,1)} %get-tuple-element.70), channel_id=1, source_target_pairs={{0,3},{1,2},{2,1},{3,0},{4,7},{5,6},{6,5},{7,4},{8,11},{9,10},{10,... | collective-permute-start | bytes 2654216 | tf_op jit(solution)/shard_map/ppermute | solution.py:167
  246.6 31.3 %collective-permute-start.10 = (bf16[4,96,1152]{2,1,0:T(8,128)(2,1)}, bf16[4,96,1152]{2,1,0:T(8,128)(2,1)S(1)}, u32[]{:S(2)}, u32[]{:S(2)}) collective-permute-start(bf16[4,96,1152]{2,1,0:T(8,128)(2,1)} %get-tuple-element.73), channel_id=1, source_target_pairs={{0,4},{1,5},{2,6},{3,7},{4,0},{5,1},{6,2},{7,3},{8,12},{9,13},{10,... | collective-permute-start | bytes 2654216 | tf_op jit(solution)/shard_map/ppermute | solution.py:167
  256.7 76.4 %collective-permute-start.13 = (bf16[4,96,1152]{2,1,0:T(8,128)(2,1)}, bf16[4,96,1152]{2,1,0:T(8,128)(2,1)}, u32[]{:S(2)}, u32[]{:S(2)}) collective-permute-start(bf16[4,96,1152]{2,1,0:T(8,128)(2,1)} %get-tuple-element.76), channel_id=1, source_target_pairs={{0,5},{1,4},{2,7},{3,6},{4,1},{5,0},{6,3},{7,2},{8,13},{9,12},{10,... | collective-permute-start | bytes 2654216 | tf_op jit(solution)/shard_map/ppermute | solution.py:167
  259.4 74.7 %collective-permute-start.16 = (bf16[4,96,1152]{2,1,0:T(8,128)(2,1)}, bf16[4,96,1152]{2,1,0:T(8,128)(2,1)}, u32[]{:S(2)}, u32[]{:S(2)}) collective-permute-start(bf16[4,96,1152]{2,1,0:T(8,128)(2,1)} %get-tuple-element.79), channel_id=1, source_target_pairs={{0,6},{1,7},{2,4},{3,5},{4,2},{5,3},{6,0},{7,1},{8,14},{9,15},{10,... | collective-permute-start | bytes 2654216 | tf_op jit(solution)/shard_map/ppermute | solution.py:167
  260.2 75.1 %collective-permute-start.19 = (bf16[4,96,1152]{2,1,0:T(8,128)(2,1)}, bf16[4,96,1152]{2,1,0:T(8,128)(2,1)}, u32[]{:S(2)}, u32[]{:S(2)}) collective-permute-start(bf16[4,96,1152]{2,1,0:T(8,128)(2,1)} %get-tuple-element.82), channel_id=1, source_target_pairs={{0,7},{1,6},{2,5},{3,4},{4,3},{5,2},{6,1},{7,0},{8,15},{9,14},{10,... | collective-permute-start | bytes 2654216 | tf_op jit(solution)/shard_map/ppermute | solution.py:167
  275.7 95.9 %collective-permute-start.8 = (bf16[6,8,1152]{2,1,0:T(8,128)(2,1)}, bf16[6,8,1152]{2,1,0:T(8,128)(2,1)}, u32[]{:S(2)}, u32[]{:S(2)}) collective-permute-start(bf16[6,8,1152]{2,1,0:T(8,128)(2,1)} %get-tuple-element.71), channel_id=1, source_target_pairs={{0,3},{1,2},{2,1},{3,0},{4,7},{5,6},{6,5},{7,4},{8,11},{9,10},{10,... | collective-permute-start | bytes 331784 | tf_op jit(solution)/shard_map/ppermute | solution.py:167
  277.9 93.7 %collective-permute-start.11 = (bf16[6,8,1152]{2,1,0:T(8,128)(2,1)}, bf16[6,8,1152]{2,1,0:T(8,128)(2,1)}, u32[]{:S(2)}, u32[]{:S(2)}) collective-permute-start(bf16[6,8,1152]{2,1,0:T(8,128)(2,1)} %get-tuple-element.74), channel_id=1, source_target_pairs={{0,4},{1,5},{2,6},{3,7},{4,0},{5,1},{6,2},{7,3},{8,12},{9,13},{10,... | collective-permute-start | bytes 331784 | tf_op jit(solution)/shard_map/ppermute | solution.py:167
  333.1 38.5 %collective-permute-start.14 = (bf16[6,8,1152]{2,1,0:T(8,128)(2,1)}, bf16[6,8,1152]{2,1,0:T(8,128)(2,1)}, u32[]{:S(2)}, u32[]{:S(2)}) collective-permute-start(bf16[6,8,1152]{2,1,0:T(8,128)(2,1)} %get-tuple-element.77), channel_id=1, source_target_pairs={{0,5},{1,4},{2,7},{3,6},{4,1},{5,0},{6,3},{7,2},{8,13},{9,12},{10,... | collective-permute-start | bytes 331784 | tf_op jit(solution)/shard_map/ppermute | solution.py:167
  334.2 37.5 %collective-permute-start.17 = (bf16[6,8,1152]{2,1,0:T(8,128)(2,1)}, bf16[6,8,1152]{2,1,0:T(8,128)(2,1)}, u32[]{:S(2)}, u32[]{:S(2)}) collective-permute-start(bf16[6,8,1152]{2,1,0:T(8,128)(2,1)} %get-tuple-element.80), channel_id=1, source_target_pairs={{0,6},{1,7},{2,4},{3,5},{4,2},{5,3},{6,0},{7,1},{8,14},{9,15},{10,... | collective-permute-start | bytes 331784 | tf_op jit(solution)/shard_map/ppermute | solution.py:167
  335.3 36.4 %collective-permute-start.20 = (bf16[6,8,1152]{2,1,0:T(8,128)(2,1)}, bf16[6,8,1152]{2,1,0:T(8,128)(2,1)}, u32[]{:S(2)}, u32[]{:S(2)}) collective-permute-start(bf16[6,8,1152]{2,1,0:T(8,128)(2,1)} %get-tuple-element.83), channel_id=1, source_target_pairs={{0,7},{1,6},{2,5},{3,4},{4,3},{5,2},{6,1},{7,0},{8,15},{9,14},{10,... | collective-permute-start | bytes 331784 | tf_op jit(solution)/shard_map/ppermute | solution.py:167
  (59 other events, 3270.9 us)
